TPU v7x, 32 devices: a whole 2x2x4 slice. The times are simulated.
32 devices in a mesh: rep: 2 (over y), blk: 8 (over z, x), head: 2 (over core).
Axes of the slice: x: 2, y: 2, z: 4, core: 2. Of those that a mesh axis runs over, the one named last changes fastest.
Arguments:
- queries: bfloat16 [2, 512, 8192], P('rep', 'blk', 'head'), parts along dimension 0, may hold values from -200 to 200
- keys: bfloat16 [2, 512, 512], P('rep', 'blk', 'head'), parts along dimension 0, may hold values from -6 to 6
- values: bfloat16 [2, 512, 512], P('rep', 'blk', 'head'), parts along dimension 0, may hold values from -6 to 6
- prompt_length: int32 [2], P('rep'), parts along dimension 0, may hold values from 256 to 512
- span_order: int32 [32], P('rep'), parts along dimension 0, may hold values from 0 to 15, as said below
Outputs:
- attended: bfloat16 [2, 512, 8192], P('rep', 'blk', 'head'), parts along dimension 0
There are 2 independent parts, one for each index of `rep`. A program takes and returns all parts, laid end to end along the dimension named above; each array names one. Nothing has to cross between parts.
Inputs may be any that keep to these rules, and one draw needn't show every extreme that they name: `span_order`: each of the 16 span numbers stands in exactly one slot.
All inputs are finite; a program needn't handle non-finite values.
Results may differ from a plain program's by a relative error of at most 0.0065.
Values may be sent and summed in bfloat16 or wider, within the bound.
A program may use at most 64 MiB of HBM per device.

v0:
```python
import jax
import jax.numpy as jnp
from jax import lax
from jax.sharding import PartitionSpec as P

HEAD_WIDTH = 128


NEG_FILL = -1e30


def from_behind(block, axis, distance):
    devices = range(lax.axis_size(axis))
    route = [((i - distance) % len(devices), i) for i in devices]
    return lax.ppermute(block, axis, route)


def shards(queries, keys, values, prompt_length, span_order):
    blocks = lax.axis_size("blk")
    mine = lax.axis_index("blk")
    prompts = queries.shape[0]
    tok_rows = queries.shape[1]
    span = tok_rows // 2
    local_heads = keys.shape[2] // HEAD_WIDTH
    group = queries.shape[2] // (local_heads * HEAD_WIDTH)
    offsets = jnp.arange(span, dtype=jnp.int32)
    all_pos = (span_order[:, None] * span + offsets[None, :]).reshape(-1)
    my_pos = lax.dynamic_slice_in_dim(all_pos, mine * tok_rows, tok_rows)
    row_pos = jnp.tile(my_pos, group)
    highest = jnp.max(my_pos)
    q_cols = (
        queries.reshape(prompts, tok_rows, local_heads, group, HEAD_WIDTH)
        .transpose(0, 2, 4, 3, 1)
        .reshape(prompts, local_heads, HEAD_WIDTH, group * tok_rows)
    )
    scale = HEAD_WIDTH ** (-0.5)

    def attend(carry, key_rows, value_rows, key_pos):
        best, total, accum = carry
        count = key_rows.shape[1]
        key_four = key_rows.reshape(prompts, count, local_heads, HEAD_WIDTH)
        value_four = value_rows.reshape(prompts, count, local_heads, HEAD_WIDTH)
        scores = (
            jnp.einsum("skhd,shdr->shkr", key_four, q_cols, preferred_element_type=jnp.float32)
            * scale
        )
        allowed = (key_pos[None, :, None] <= row_pos[None, None, :]) & (
            key_pos[None, :, None] < prompt_length[:, None, None]
        )
        scores = jnp.where(allowed[:, None], scores, NEG_FILL)
        fresh = jnp.maximum(best, jnp.max(scores, axis=2))
        weights = jnp.where(allowed[:, None], jnp.exp(scores - fresh[:, :, None, :]), 0.0)
        factor = jnp.exp(best - fresh)
        total = total * factor + jnp.sum(weights, axis=2)
        mixed = jnp.einsum(
            "shkr,skhd->shrd",
            weights.astype(jnp.bfloat16),
            value_four,
            preferred_element_type=jnp.float32,
        )
        accum = accum * factor[..., None] + mixed
        return (fresh, total, accum)

    def visit(carry, key_rows, value_rows, key_pos):
        live = jnp.any((key_pos[None, :] <= highest) & (key_pos[None, :] < prompt_length[:, None]))
        return lax.cond(
            live,
            lambda state: attend(state, key_rows, value_rows, key_pos),
            lambda state: state,
            carry,
        )

    width = group * tok_rows
    init = (
        jnp.full((prompts, local_heads, width), NEG_FILL, jnp.float32),
        jnp.zeros((prompts, local_heads, width), jnp.float32),
        jnp.zeros((prompts, local_heads, width, HEAD_WIDTH), jnp.float32),
    )
    paired = jnp.stack([keys, values])

    def pass_forward(block):
        return from_behind(block, "blk", 1)

    def source_pos(source):
        return lax.dynamic_slice_in_dim(all_pos, source * tok_rows, tok_rows)

    carry = visit(init, keys, values, my_pos)

    def turn(step, state):
        carry, ahead, behind = state
        ahead = pass_forward(ahead)
        behind = from_behind(behind, "blk", -1)
        pos_ahead = source_pos((mine - step) % blocks)
        pos_behind = source_pos((mine + step) % blocks)
        carry = visit(
            carry,
            jnp.concatenate([ahead[0], behind[0]], axis=1),
            jnp.concatenate([ahead[1], behind[1]], axis=1),
            jnp.concatenate([pos_ahead, pos_behind]),
        )
        return (carry, ahead, behind)

    carry, ahead, behind = lax.fori_loop(1, blocks // 2, turn, (carry, paired, paired))
    ahead = pass_forward(ahead)
    carry = visit(carry, ahead[0], ahead[1], source_pos((mine - blocks // 2) % blocks))
    best, total, accum = carry
    normed = accum / total[..., None]
    joined_heads = (
        normed.reshape(prompts, local_heads, group, tok_rows, HEAD_WIDTH)
        .transpose(0, 3, 1, 2, 4)
        .reshape(prompts, tok_rows, local_heads * group * HEAD_WIDTH)
    )
    joined_heads = jnp.where(
        (my_pos[None, :] < prompt_length[:, None])[:, :, None], joined_heads, 0.0
    )
    return joined_heads.astype(jnp.bfloat16)


def solution(mesh):
    in_specs = (
        P("rep", "blk", "head"),
        P("rep", "blk", "head"),
        P("rep", "blk", "head"),
        P("rep"),
        P("rep"),
    )
    out_specs = P("rep", "blk", "head")
    return jax.shard_map(shards, mesh=mesh, in_specs=in_specs, out_specs=out_specs, check_vma=False)
```

profile of v0, /device:TPU:0, one launch (start us, length us, event | category | flops | bytes accessed | tf_op | source)
XLA Modules:
  0.0 67.7 jit_solution(15494096809249109004)
XLA Ops:
  2.7 1.2 %and_reduce_fusion.1 = pred[]{:T(512)} fusion(s32[64]{0:T(128)S(1)} %get-tuple-element.662, s32[]{:T(128)} %reduce_max.40, s32[]{:T(128)} %bitcast.103), kind=kLoop, calls=%fused_computation.75 | loop fusion | flops 255 | bytes 265 | tf_op jit(solution)/shard_map/reduce_or | solution.py:65
  4.6 1.1 %copy.37 = bf16[8,8,32,128]{3,2,1,0:T(8,128)(2,1)S(1)} copy(bf16[8,8,32,128]{3,1,2,0:T(8,128)(2,1)} %bitcast.112) | data formatting | bytes 1048576
  6.8 2.5 %conditional.3 = (f32[1,2,1024]{2,1,0:T(2,128)S(1)}, f32[1,2,1024]{2,1,0:T(2,128)}, f32[1,2,1024,128]{3,2,1,0:T(8,128)S(1)}) conditional(s32[]{:T(128)} %convert_element_type.40, () %tuple.49, (s32[64]{0:T(128)S(1)}, s32[16,64]{1,0:T(8,128)S(1)}, s32[1]{0:T(128)}, bf16[1,64,256]{2,1,0:T(8,128)(2,1)S(1)}, bf16[1,2,128,1024]{2,3,1,0:T(8,128)(2,1)S(1)}, ...), branch_computations={%region_3.4_spmd, %region_4.7_spmd} | conditional | flops 68692032 | bytes 3715740 | solution.py:66
  9.3 44.6 %while.24 = (s32[]{:T(128)}, f32[1,2,1024]{2,1,0:T(2,128)S(1)}, f32[1,2,1024]{2,1,0:T(2,128)}, f32[1,2,1024,128]{3,2,1,0:T(8,128)S(1)}, bf16[2,1,64,256]{3,2,1,0...) while((s32[]{:T(128)}, f32[1,2,1024]{2,1,0:T(2,128)S(1)}, ...), condition=%wide.region_13.14_spmd.clone, body=%wide.region_7.13_spmd.clone.sunk | while | flops 137632672 | bytes 8199017 | solution.py:103
  9.3 6.0 %collective-permute-start = (bf16[2,1,64,256]{3,2,1,0:T(8,128)(2,1)S(1)}, bf16[2,1,64,256]{3,2,1,0:T(8,128)(2,1)S(1)}, u32[]{:S(2)}, u32[]{:S(2)}) collective-permute-start(bf16[2,1,64,256]{3,2,1,0:T(8,128)(2,1)S(1)} %get-tuple-element.674), channel_id=1, source_target_pairs={{2,0},{4,2},{6,4},{8,6},{10,8},{12,10},{14,12},{0,14},{3,1},{5,3},... | collective-permute-start | bytes 196616 | tf_op jit(solution)/shard_map/while/body/eval_jaxpr/ppermute | solution.py:15
  15.4 2.0 %and_reduce_fusion.4 = pred[]{:T(512)} fusion(s32[1,64]{1,0:T(1,128)S(1)} %bitcast.116, s32[1,64]{1,0:T(1,128)S(1)} %bitcast.115, s32[]{:T(128)} %bitcast.100, s32[]{:T(128)} %get-tuple-element.695), kind=kLoop, calls=%fused_computation.68.clone.1 | loop fusion | flops 639 | bytes 521 | tf_op jit(solution)/shard_map/while/body/eval_jaxpr/reduce_or | solution.py:65
  18.2 4.1 %collective-permute-done.1 = bf16[2,1,64,256]{3,2,1,0:T(8,128)(2,1)S(1)} collective-permute-done((bf16[2,1,64,256]{3,2,1,0:T(8,128)(2,1)S(1)}, bf16[2,1,64,256]{3,2,1,0:T(8,128)(2,1)S(1)}, u32[]{:S(2)}, u32[]{:S(2)}) %collective-permute-start.1) | collective-permute-done | bytes 65568 | tf_op jit(solution)/shard_map/while/body/eval_jaxpr/ppermute | solution.py:15
  22.3 4.9 %conditional.7 = ((f32[1,2,1024]{2,1,0:T(2,128)S(1)}, f32[1,2,1024]{2,1,0:T(2,128)}, f32[1,2,1024,128]{3,2,1,0:T(8,128)S(1)})) conditional(s32[]{:T(128)} %convert_element_type.51, (f32[1,2,1024]{2,1,0:T(2,128)S(1)}, f32[1,2,1024]{2,1,0:T(2,128)}, f32[1,2,1024,128]{3,2,1,0:T(8,128)S(1)}) %tuple.97, (s32[128]{0:T(128)S(1)}, s32[64]{0:T(128)S(1)}, ...), branch_computations={%region_9.9_spmd, %region_10.12_spmd} | conditional | flops 137369728 | bytes 6866496 | solution.py:66
  24.5 1.3 %bitcast_add_fusion.1 = f32[1,2,1024]{2,1,0:T(2,128)} fusion(f32[2,1024]{1,0:T(2,128)S(1)} %fusion.18, f32[1,2,1024]{2,1,0:T(2,128)} %get-tuple-element.364, f32[1,2,1024]{2,1,0:T(2,128)S(1)} %get-tuple-element.358, f32[1,2,1024]{2,1,0:T(2,128)S(1)} %get-tuple-element.642), kind=kLoop, calls=%fused_computation.35 | loop fusion | flops 6144 | bytes 40960 | tf_op jit(solution)/shard_map/while/body/eval_jaxpr/cond/branch_1_fun/add | solution.py:54
  27.9 2.0 %collective-permute-start.1 = (bf16[2,1,64,256]{3,2,1,0:T(8,128)(2,1)S(1)}, bf16[2,1,64,256]{3,2,1,0:T(8,128)(2,1)S(1)}, u32[]{:S(2)}, u32[]{:S(2)}) collective-permute-start(bf16[2,1,64,256]{3,2,1,0:T(8,128)(2,1)S(1)} %get-tuple-element.673), channel_id=1, source_target_pairs={{14,0},{0,2},{2,4},{4,6},{6,8},{8,10},{10,12},{12,14},{15,1},{1,3}... | collective-permute-start | bytes 196616 | tf_op jit(solution)/shard_map/while/body/eval_jaxpr/ppermute | solution.py:15
  30.0 2.0 %and_reduce_fusion.4 = pred[]{:T(512)} fusion(s32[1,64]{1,0:T(1,128)S(1)} %bitcast.116, s32[1,64]{1,0:T(1,128)S(1)} %bitcast.115, s32[]{:T(128)} %bitcast.100, s32[]{:T(128)} %get-tuple-element.695), kind=kLoop, calls=%fused_computation.68.clone.1 | loop fusion | flops 639 | bytes 521 | tf_op jit(solution)/shard_map/while/body/eval_jaxpr/reduce_or | solution.py:65
  32.9 2.0 %collective-permute-done.1 = bf16[2,1,64,256]{3,2,1,0:T(8,128)(2,1)S(1)} collective-permute-done((bf16[2,1,64,256]{3,2,1,0:T(8,128)(2,1)S(1)}, bf16[2,1,64,256]{3,2,1,0:T(8,128)(2,1)S(1)}, u32[]{:S(2)}, u32[]{:S(2)}) %collective-permute-start.1) | collective-permute-done | bytes 65568 | tf_op jit(solution)/shard_map/while/body/eval_jaxpr/ppermute | solution.py:15
  35.0 4.9 %conditional.7 = ((f32[1,2,1024]{2,1,0:T(2,128)S(1)}, f32[1,2,1024]{2,1,0:T(2,128)}, f32[1,2,1024,128]{3,2,1,0:T(8,128)S(1)})) conditional(s32[]{:T(128)} %convert_element_type.51, (f32[1,2,1024]{2,1,0:T(2,128)S(1)}, f32[1,2,1024]{2,1,0:T(2,128)}, f32[1,2,1024,128]{3,2,1,0:T(8,128)S(1)}) %tuple.97, (s32[128]{0:T(128)S(1)}, s32[64]{0:T(128)S(1)}, ...), branch_computations={%region_9.9_spmd, %region_10.12_spmd} | conditional | flops 137369728 | bytes 6866496 | solution.py:66
  37.1 1.3 %bitcast_add_fusion.1 = f32[1,2,1024]{2,1,0:T(2,128)} fusion(f32[2,1024]{1,0:T(2,128)S(1)} %fusion.18, f32[1,2,1024]{2,1,0:T(2,128)} %get-tuple-element.364, f32[1,2,1024]{2,1,0:T(2,128)S(1)} %get-tuple-element.358, f32[1,2,1024]{2,1,0:T(2,128)S(1)} %get-tuple-element.642), kind=kLoop, calls=%fused_computation.35 | loop fusion | flops 6144 | bytes 40960 | tf_op jit(solution)/shard_map/while/body/eval_jaxpr/cond/branch_1_fun/add | solution.py:54
  41.2 1.4 %collective-permute-start.1 = (bf16[2,1,64,256]{3,2,1,0:T(8,128)(2,1)S(1)}, bf16[2,1,64,256]{3,2,1,0:T(8,128)(2,1)S(1)}, u32[]{:S(2)}, u32[]{:S(2)}) collective-permute-start(bf16[2,1,64,256]{3,2,1,0:T(8,128)(2,1)S(1)} %get-tuple-element.673), channel_id=1, source_target_pairs={{14,0},{0,2},{2,4},{4,6},{6,8},{8,10},{10,12},{12,14},{15,1},{1,3}... | collective-permute-start | bytes 196616 | tf_op jit(solution)/shard_map/while/body/eval_jaxpr/ppermute | solution.py:15
  42.7 2.0 %and_reduce_fusion.4 = pred[]{:T(512)} fusion(s32[1,64]{1,0:T(1,128)S(1)} %bitcast.116, s32[1,64]{1,0:T(1,128)S(1)} %bitcast.115, s32[]{:T(128)} %bitcast.100, s32[]{:T(128)} %get-tuple-element.695), kind=kLoop, calls=%fused_computation.68.clone.1 | loop fusion | flops 639 | bytes 521 | tf_op jit(solution)/shard_map/while/body/eval_jaxpr/reduce_or | solution.py:65
  45.6 2.6 %collective-permute-done.1 = bf16[2,1,64,256]{3,2,1,0:T(8,128)(2,1)S(1)} collective-permute-done((bf16[2,1,64,256]{3,2,1,0:T(8,128)(2,1)S(1)}, bf16[2,1,64,256]{3,2,1,0:T(8,128)(2,1)S(1)}, u32[]{:S(2)}, u32[]{:S(2)}) %collective-permute-start.1) | collective-permute-done | bytes 65568 | tf_op jit(solution)/shard_map/while/body/eval_jaxpr/ppermute | solution.py:15
  48.2 4.9 %conditional.7 = ((f32[1,2,1024]{2,1,0:T(2,128)S(1)}, f32[1,2,1024]{2,1,0:T(2,128)}, f32[1,2,1024,128]{3,2,1,0:T(8,128)S(1)})) conditional(s32[]{:T(128)} %convert_element_type.51, (f32[1,2,1024]{2,1,0:T(2,128)S(1)}, f32[1,2,1024]{2,1,0:T(2,128)}, f32[1,2,1024,128]{3,2,1,0:T(8,128)S(1)}) %tuple.97, (s32[128]{0:T(128)S(1)}, s32[64]{0:T(128)S(1)}, ...), branch_computations={%region_9.9_spmd, %region_10.12_spmd} | conditional | flops 137369728 | bytes 6866496 | solution.py:66
  50.4 1.3 %bitcast_add_fusion.1 = f32[1,2,1024]{2,1,0:T(2,128)} fusion(f32[2,1024]{1,0:T(2,128)S(1)} %fusion.18, f32[1,2,1024]{2,1,0:T(2,128)} %get-tuple-element.364, f32[1,2,1024]{2,1,0:T(2,128)S(1)} %get-tuple-element.358, f32[1,2,1024]{2,1,0:T(2,128)S(1)} %get-tuple-element.642), kind=kLoop, calls=%fused_computation.35 | loop fusion | flops 6144 | bytes 40960 | tf_op jit(solution)/shard_map/while/body/eval_jaxpr/cond/branch_1_fun/add | solution.py:54
  53.9 1.3 %and_reduce_fusion.2 = (pred[]{:T(512)}, s32[64]{0:T(128)S(1)}) fusion(s32[]{:T(128)} %reduce_max.40, s32[]{:T(128)} %bitcast.102, s32[512]{0:T(512)S(1)} %get-tuple-element.720, s32[]{:T(128)S(6)} %select_n.101), kind=kLoop, calls=%fused_computation.76 | loop fusion | flops 255 | bytes 525 | tf_op jit(solution)/shard_map/reduce_or | solution.py:65
  55.8 5.0 %collective-permute-done.2 = bf16[2,1,64,256]{3,2,1,0:T(8,128)(2,1)S(1)} collective-permute-done((bf16[2,1,64,256]{3,2,1,0:T(8,128)(2,1)S(1)}, bf16[2,1,64,256]{3,2,1,0:T(8,128)(2,1)S(1)}, u32[]{:S(2)}, u32[]{:S(2)}) %collective-permute-start.2) | collective-permute-done | bytes 65568 | tf_op jit(solution)/shard_map/ppermute | solution.py:15
  60.8 3.7 %conditional.4 = ((f32[1,2,1024]{2,1,0:T(2,128)}, f32[1,2,1024,128]{3,2,1,0:T(8,128)S(1)})) conditional(s32[]{:T(128)} %convert_element_type.39, (f32[1,2,1024]{2,1,0:T(2,128)}, f32[1,2,1024,128]{3,2,1,0:T(8,128)S(1)}) %tuple.52, (s32[64]{0:T(128)S(1)}, s32[16,64]{1,0:T(8,128)S(1)}, s32[1]{0:T(128)}, bf16[2,1,64,256]{3,2,1,0:T(8,128)(2,1)S(1)}, ...), branch_computations={%region_14.15_spmd, %region_15.18_spmd} | conditional | flops 68952128 | bytes 4911772 | solution.py:66
  63.2 1.3 %bitcast_add_fusion.2 = f32[1,2,1024]{2,1,0:T(2,128)} fusion(f32[2,1024]{1,0:T(2,128)S(1)} %fusion.32, f32[1,2,1024]{2,1,0:T(2,128)} %get-tuple-element.383, f32[1,2,1024]{2,1,0:T(2,128)S(1)} %get-tuple-element.384, f32[2,1024]{1,0:T(2,128)S(1)} %get-tuple-element.528), kind=kLoop, calls=%fused_computation.55 | loop fusion | flops 8192 | bytes 40960 | tf_op jit(solution)/shard_map/cond/branch_1_fun/add | solution.py:54
  64.5 1.0 %broadcast_divide_fusion = bf16[1,2,1024,128]{3,2,1,0:T(8,128)(2,1)S(1)} fusion(f32[1,2,1024,128]{3,2,1,0:T(8,128)S(1)} %get-tuple-element.407, f32[2,1024]{1,0:T(2,128)} %bitcast.24), kind=kLoop, calls=%fused_computation.72 | loop fusion | flops 524288 | bytes 1581056 | tf_op jit(solution)/shard_map/div | solution.py:107
  (136 shorter events, 24.0 us)
Async XLA Ops:
  0.0 0.7 copy-start.10
  5.9 0.8 %copy-start.1 = (bf16[1,64,256]{2,1,0:T(8,128)(2,1)S(1)}, bf16[1,64,256]{2,1,0:T(8,128)(2,1)}, u32[]{:S(2)}) copy-start(bf16[1,64,256]{2,1,0:T(8,128)(2,1)} %param.14) | copy-start | bytes 98308
  5.9 0.8 %copy-start.2 = (bf16[1,64,256]{2,1,0:T(8,128)(2,1)S(1)}, bf16[1,64,256]{2,1,0:T(8,128)(2,1)}, u32[]{:S(2)}) copy-start(bf16[1,64,256]{2,1,0:T(8,128)(2,1)} %param.15) | copy-start | bytes 98308
  9.3 6.0 %copy-start.7 = (s32[512]{0:T(512)}, s32[512]{0:T(512)S(1)}, u32[]{:S(2)}) copy-start(s32[512]{0:T(512)S(1)} %get-tuple-element.694) | copy-start | bytes 6148 | tf_op jit(solution)/shard_map/while
  9.3 13.0 %copy-start.5 = (s32[64]{0:T(128)}, s32[64]{0:T(128)S(1)}, u32[]{:S(2)}) copy-start(s32[64]{0:T(128)S(1)} %get-tuple-element.698) | copy-start | bytes 772 | tf_op jit(solution)/shard_map/while
  9.3 8.8 %collective-permute-start = (bf16[2,1,64,256]{3,2,1,0:T(8,128)(2,1)S(1)}, bf16[2,1,64,256]{3,2,1,0:T(8,128)(2,1)S(1)}, u32[]{:S(2)}, u32[]{:S(2)}) collective-permute-start(bf16[2,1,64,256]{3,2,1,0:T(8,128)(2,1)S(1)} %get-tuple-element.674), channel_id=1, source_target_pairs={{2,0},{4,2},{6,4},{8,6},{10,8},{12,10},{14,12},{0,14},{3,1},{5,3},... | collective-permute-start | bytes 196616 | tf_op jit(solution)/shard_map/while/body/eval_jaxpr/ppermute | solution.py:15
  15.3 7.0 %collective-permute-start.1 = (bf16[2,1,64,256]{3,2,1,0:T(8,128)(2,1)S(1)}, bf16[2,1,64,256]{3,2,1,0:T(8,128)(2,1)S(1)}, u32[]{:S(2)}, u32[]{:S(2)}) collective-permute-start(bf16[2,1,64,256]{3,2,1,0:T(8,128)(2,1)S(1)} %get-tuple-element.673), channel_id=1, source_target_pairs={{14,0},{0,2},{2,4},{4,6},{6,8},{8,10},{10,12},{12,14},{15,1},{1,3}... | collective-permute-start | bytes 196616 | tf_op jit(solution)/shard_map/while/body/eval_jaxpr/ppermute | solution.py:15
  25.8 0.7 %copy-start = (f32[2,1024]{1,0:T(2,128)S(1)}, f32[2,1024]{1,0:T(2,128)}, u32[]{:S(2)}) copy-start(f32[2,1024]{1,0:T(2,128)} %get-tuple-element.518) | copy-start | bytes 24580 | tf_op jit(solution)/shard_map/while/body/eval_jaxpr/cond
  27.3 0.7 copy-start.8
  27.9 2.0 %copy-start.7 = (s32[512]{0:T(512)}, s32[512]{0:T(512)S(1)}, u32[]{:S(2)}) copy-start(s32[512]{0:T(512)S(1)} %get-tuple-element.694) | copy-start | bytes 6148 | tf_op jit(solution)/shard_map/while
  27.9 7.0 %copy-start.5 = (s32[64]{0:T(128)}, s32[64]{0:T(128)S(1)}, u32[]{:S(2)}) copy-start(s32[64]{0:T(128)S(1)} %get-tuple-element.698) | copy-start | bytes 772 | tf_op jit(solution)/shard_map/while
  27.9 5.0 %collective-permute-start = (bf16[2,1,64,256]{3,2,1,0:T(8,128)(2,1)S(1)}, bf16[2,1,64,256]{3,2,1,0:T(8,128)(2,1)S(1)}, u32[]{:S(2)}, u32[]{:S(2)}) collective-permute-start(bf16[2,1,64,256]{3,2,1,0:T(8,128)(2,1)S(1)} %get-tuple-element.674), channel_id=1, source_target_pairs={{2,0},{4,2},{6,4},{8,6},{10,8},{12,10},{14,12},{0,14},{3,1},{5,3},... | collective-permute-start | bytes 196616 | tf_op jit(solution)/shard_map/while/body/eval_jaxpr/ppermute | solution.py:15
  27.9 7.0 %collective-permute-start.1 = (bf16[2,1,64,256]{3,2,1,0:T(8,128)(2,1)S(1)}, bf16[2,1,64,256]{3,2,1,0:T(8,128)(2,1)S(1)}, u32[]{:S(2)}, u32[]{:S(2)}) collective-permute-start(bf16[2,1,64,256]{3,2,1,0:T(8,128)(2,1)S(1)} %get-tuple-element.673), channel_id=1, source_target_pairs={{14,0},{0,2},{2,4},{4,6},{6,8},{8,10},{10,12},{12,14},{15,1},{1,3}... | collective-permute-start | bytes 196616 | tf_op jit(solution)/shard_map/while/body/eval_jaxpr/ppermute | solution.py:15
  38.5 0.7 %copy-start = (f32[2,1024]{1,0:T(2,128)S(1)}, f32[2,1024]{1,0:T(2,128)}, u32[]{:S(2)}) copy-start(f32[2,1024]{1,0:T(2,128)} %get-tuple-element.518) | copy-start | bytes 24580 | tf_op jit(solution)/shard_map/while/body/eval_jaxpr/cond
  40.0 0.7 copy-start.8
  40.0 0.6 copy-start.6
  40.6 2.0 %copy-start.7 = (s32[512]{0:T(512)}, s32[512]{0:T(512)S(1)}, u32[]{:S(2)}) copy-start(s32[512]{0:T(512)S(1)} %get-tuple-element.694) | copy-start | bytes 6148 | tf_op jit(solution)/shard_map/while
  40.6 7.6 %copy-start.5 = (s32[64]{0:T(128)}, s32[64]{0:T(128)S(1)}, u32[]{:S(2)}) copy-start(s32[64]{0:T(128)S(1)} %get-tuple-element.698) | copy-start | bytes 772 | tf_op jit(solution)/shard_map/while
  40.6 5.0 %collective-permute-start = (bf16[2,1,64,256]{3,2,1,0:T(8,128)(2,1)S(1)}, bf16[2,1,64,256]{3,2,1,0:T(8,128)(2,1)S(1)}, u32[]{:S(2)}, u32[]{:S(2)}) collective-permute-start(bf16[2,1,64,256]{3,2,1,0:T(8,128)(2,1)S(1)} %get-tuple-element.674), channel_id=1, source_target_pairs={{2,0},{4,2},{6,4},{8,6},{10,8},{12,10},{14,12},{0,14},{3,1},{5,3},... | collective-permute-start | bytes 196616 | tf_op jit(solution)/shard_map/while/body/eval_jaxpr/ppermute | solution.py:15
  41.2 7.0 %collective-permute-start.1 = (bf16[2,1,64,256]{3,2,1,0:T(8,128)(2,1)S(1)}, bf16[2,1,64,256]{3,2,1,0:T(8,128)(2,1)S(1)}, u32[]{:S(2)}, u32[]{:S(2)}) collective-permute-start(bf16[2,1,64,256]{3,2,1,0:T(8,128)(2,1)S(1)} %get-tuple-element.673), channel_id=1, source_target_pairs={{14,0},{0,2},{2,4},{4,6},{6,8},{8,10},{10,12},{12,14},{15,1},{1,3}... | collective-permute-start | bytes 196616 | tf_op jit(solution)/shard_map/while/body/eval_jaxpr/ppermute | solution.py:15
  51.7 0.7 %copy-start = (f32[2,1024]{1,0:T(2,128)S(1)}, f32[2,1024]{1,0:T(2,128)}, u32[]{:S(2)}) copy-start(f32[2,1024]{1,0:T(2,128)} %get-tuple-element.518) | copy-start | bytes 24580 | tf_op jit(solution)/shard_map/while/body/eval_jaxpr/cond
  53.2 0.7 copy-start.8
  53.9 7.0 %collective-permute-start.2 = (bf16[2,1,64,256]{3,2,1,0:T(8,128)(2,1)S(1)}, bf16[2,1,64,256]{3,2,1,0:T(8,128)(2,1)S(1)}, u32[]{:S(2)}, u32[]{:S(2)}) collective-permute-start(bf16[2,1,64,256]{3,2,1,0:T(8,128)(2,1)S(1)} %get-tuple-element.405), channel_id=1, source_target_pairs={{14,0},{0,2},{2,4},{4,6},{6,8},{8,10},{10,12},{12,14},{15,1},{1,3}... | collective-permute-start | bytes 196616 | tf_op jit(solution)/shard_map/ppermute | solution.py:15
  53.9 7.0 %copy-start.4 = (s32[16,64]{1,0:T(8,128)S(1)}, s32[16,64]{1,0:T(8,128)}, u32[]{:S(2)}) copy-start(s32[16,64]{1,0:T(8,128)} %copy-done.3) | copy-start | bytes 12292
  (4 other events, 2.5 us)
where the time goes:
time: 68.1 us; the launch traced here: 67.7 us
  other arithmetic  24.6 us (36%)
  waiting for transfers between devices  14 us (21%)
  starting transfers between devices  10.1 us (15%)
  local copies, waits for them, and re-layouts  8.89 us (13%)
  matrix products  5.45 us (8%)
  loops' own time  2.56 us (4%)
  between operations  2.05 us (3%)
    ppermute x7, waiting for transfers between devices, from_behind(): return lax.ppermute(block, axis, route)  14 us
    ppermute x7, starting transfers between devices, from_behind(): return lax.ppermute(block, axis, route)  10.1 us
    reduce_or x5, other arithmetic, visit(): jnp.any((key_pos[None, :] <= highest) & (key_pos[None, :] < prompt_length...  8.43 us
    add x5, other arithmetic, attend(): total = total * factor + jnp.sum(weights, axis=2)  5.86 us
    dot_general x5, matrix products, attend(): jnp.einsum('shkr,skhd->shrd', weights.astype(jnp.bfloat16), value_four, p...  3.75 us
    lt x5, other arithmetic, attend(): key_pos[None, :, None] < prompt_length[:, None, None]  3.26 us
    unnamed x15, local copies, waits for them, and re-layouts  3.21 us
    another operation x1, loops' own time, shards(): lax.fori_loop(1, blocks // 2, turn, (carry, paired, paired))  2.24 us
  transfers between devices with their start and end apart: 7, of which 6 were waited for; matrix products, arithmetic and copies ran while one was open for 11% of the time, Pallas kernels for 0%

commit v1 on v0

v1 whole, which is shorter than its diff:
```python
import functools
import math

import jax
import jax.numpy as jnp
from jax import lax
from jax.experimental import pallas as pl
from jax.experimental.pallas import tpu as pltpu
from jax.sharding import PartitionSpec as P

HEAD_WIDTH = 128
NEG_FILL = -1e30
HEADS_PER_TILE = 4
KEY_CHUNK = 512
MESH = pl.DeviceIdType.MESH


def kernel(
    blocks, local_heads, group, spans, q_hbm, k_hbm, v_hbm, len_ref, order_ref, o_ref,
    q_ref, k_ref, v_ref, bias_ref, q_sem, own_sem, send_sem, recv_sem
):
    rows = q_ref.shape[0]
    span = rows // spans
    keys = blocks * rows
    me = lax.axis_index("blk")
    own = pl.ds(me * rows, rows)
    q_copy = pltpu.make_async_copy(q_hbm.at[0], q_ref, q_sem)
    k_copy = pltpu.make_async_copy(k_hbm.at[0], k_ref.at[own], own_sem.at[0])
    v_copy = pltpu.make_async_copy(v_hbm.at[0], v_ref.at[own], own_sem.at[1])
    k_copy.start()
    v_copy.start()
    q_copy.start()

    barrier = pltpu.get_barrier_semaphore()
    for d in range(1, blocks):
        pl.semaphore_signal(
            barrier, inc=1, device_id={"blk": lax.rem(me + d, blocks)}, device_id_type=MESH
        )
    pl.semaphore_wait(barrier, blocks - 1)

    def send(ref, which, d):
        return pltpu.make_async_remote_copy(
            src_ref=ref.at[own],
            dst_ref=ref.at[own],
            send_sem=send_sem.at[which, d - 1],
            recv_sem=recv_sem.at[which, d - 1],
            device_id={"blk": lax.rem(me + d, blocks)},
            device_id_type=MESH,
        )

    def arrival(ref, which, d):
        source = lax.rem(me + blocks - d, blocks)
        there = pl.ds(source * rows, rows)
        return pltpu.make_async_remote_copy(
            src_ref=ref.at[there],
            dst_ref=ref.at[there],
            send_sem=send_sem.at[which, d - 1],
            recv_sem=recv_sem.at[which, d - 1],
            device_id={"blk": lax.rem(me + d, blocks)},
            device_id_type=MESH,
        )

    k_copy.wait()
    for d in range(1, blocks):
        send(k_ref, 0, d).start()
    v_copy.wait()
    for d in range(1, blocks):
        send(v_ref, 1, d).start()

    limit = len_ref[0]
    row = lax.broadcasted_iota(jnp.int32, (rows, 1), 0)
    row_pos = jnp.zeros((rows, 1), jnp.int32)
    for t in range(spans):
        row_pos = jnp.where(row // span == t, order_ref[me * spans + t] * span + row % span, row_pos)
    chunk = min(keys, KEY_CHUNK)
    chunks = keys // chunk
    lane = lax.broadcasted_iota(jnp.int32, (1, chunk), 1)

    def make_bias(c):
        key_pos = jnp.zeros((1, chunk), jnp.int32)
        for t in range(chunk // span):
            key_pos = jnp.where(
                lane // span == t, order_ref[c * (chunk // span) + t] * span + lane % span, key_pos
            )
        allowed = (key_pos <= row_pos) & (key_pos < limit)
        bias_ref[c] = jnp.where(allowed, 0.0, NEG_FILL)

    pl.loop(0, chunks)(make_bias)
    live = row_pos < limit
    q_copy.wait()

    for which, ref in ((0, k_ref), (1, v_ref)):
        for d in range(1, blocks):
            arrival(ref, which, d).wait_recv()

    scale = HEAD_WIDTH ** (-0.5) * math.log2(math.e)
    tile = HEADS_PER_TILE if group % HEADS_PER_TILE == 0 else 1
    height = tile * rows
    ones = jnp.ones((chunk, HEAD_WIDTH), jnp.bfloat16)

    for h in range(local_heads):
        cols = slice(h * HEAD_WIDTH, (h + 1) * HEAD_WIDTH)

        def run_tile(i, h=h, cols=cols):
            first = h * group * HEAD_WIDTH + i * (tile * HEAD_WIDTH)

            def q_cols(t):
                return pl.ds(pl.multiple_of(first + t * HEAD_WIDTH, HEAD_WIDTH), HEAD_WIDTH)

            q = jnp.concatenate([q_ref[:, q_cols(t)] for t in range(tile)], axis=0)

            def part(c):
                at = pl.ds(pl.multiple_of(c * chunk, chunk), chunk)
                score = lax.dot_general(
                    q, k_ref[at, cols], (((1,), (1,)), ((), ())), preferred_element_type=jnp.float32
                )
                score = (score * scale).reshape(tile, rows, chunk) + bias_ref[c][None]
                return score.reshape(height, chunk), jnp.concatenate([v_ref[at, cols], ones], axis=1)

            if chunks == 1:
                score, value = part(0)
                top = jnp.max(score, axis=1, keepdims=True)
                weight = jnp.exp2(score - top).astype(jnp.bfloat16)
                mixed = jnp.dot(weight, value, preferred_element_type=jnp.float32)
            else:

                def step(c, state):
                    best, mixed = state
                    score, value = part(c)
                    top = jnp.maximum(best, jnp.max(score, axis=1, keepdims=True))
                    weight = jnp.exp2(score - top).astype(jnp.bfloat16)
                    fresh = jnp.dot(weight, value, preferred_element_type=jnp.float32)
                    return top, mixed * jnp.exp2(best - top) + fresh

                init = (
                    jnp.full((height, 1), NEG_FILL, jnp.float32),
                    jnp.zeros((height, 2 * HEAD_WIDTH), jnp.float32),
                )
                _, mixed = lax.fori_loop(0, chunks, step, init)
            out = mixed[:, :HEAD_WIDTH] / mixed[:, HEAD_WIDTH:]
            for t in range(tile):
                piece = jnp.where(live, out[t * rows : (t + 1) * rows], 0.0)
                o_ref[0, :, q_cols(t)] = piece.astype(o_ref.dtype)

        pl.loop(0, group // tile)(run_tile)

    for which, ref in ((0, k_ref), (1, v_ref)):
        for d in range(1, blocks):
            send(ref, which, d).wait_send()


def solution(mesh):
    blocks = mesh.shape["blk"]

    def shards(queries, keys, values, prompt_length, span_order):
        _, rows, width = queries.shape
        kv_width = keys.shape[2]
        local_heads = kv_width // HEAD_WIDTH
        group = width // kv_width
        total = blocks * rows
        chunk = min(total, KEY_CHUNK)
        anywhere = pl.BlockSpec(memory_space=pl.ANY)
        scalars = pl.BlockSpec(memory_space=pltpu.SMEM)
        return pl.pallas_call(
            functools.partial(kernel, blocks, local_heads, group, span_order.shape[0] // blocks),
            out_shape=jax.ShapeDtypeStruct(queries.shape, queries.dtype),
            in_specs=[anywhere, anywhere, anywhere, scalars, scalars],
            out_specs=pl.BlockSpec(memory_space=pltpu.VMEM),
            scratch_shapes=[
                pltpu.VMEM((rows, width), queries.dtype),
                pltpu.VMEM((total, kv_width), keys.dtype),
                pltpu.VMEM((total, kv_width), values.dtype),
                pltpu.VMEM((total // chunk, rows, chunk), jnp.float32),
                pltpu.SemaphoreType.DMA,
                pltpu.SemaphoreType.DMA((2,)),
                pltpu.SemaphoreType.DMA((2, blocks - 1)),
                pltpu.SemaphoreType.DMA((2, blocks - 1)),
            ],
            compiler_params=pltpu.CompilerParams(
                collective_id=0, has_side_effects=True, vmem_limit_bytes=56 * 1024 * 1024
            ),
        )(queries, keys, values, prompt_length, span_order)

    spec = P("rep", "blk", "head")
    return jax.shard_map(
        shards, mesh=mesh, in_specs=(spec, spec, spec, P("rep"), P("rep")), out_specs=spec, check_vma=False
    )
```

time: 68.1 us -> 25.9 us (0.38)
  other arithmetic: 24.6 us -> 0 us
  Pallas kernels: 0 us -> 23.2 us
  waiting for transfers between devices: 14 us -> 0 us
  starting transfers between devices: 10.1 us -> 0 us
  local copies, waits for them, and re-layouts: 8.89 us -> 1.87 us
  matrix products: 5.45 us -> 0 us
  loops' own time: 2.56 us -> 0 us
  between operations: 2.05 us -> 0.66 us
    pallas_call x0 -> x1, Pallas kernels: none -> 23.2 us  [shards(): pl.pallas_call(functools.partial(kernel, blocks, local_heads, group, span...]
    ppermute x7 -> x0, waiting for transfers between devices: 14 us -> none  [from_behind(): return lax.ppermute(block, axis, route)]
    ppermute x7 -> x0, starting transfers between devices: 10.1 us -> none  [from_behind(): return lax.ppermute(block, axis, route)]
    reduce_or x5 -> x0, other arithmetic: 8.43 us -> none  [visit(): jnp.any((key_pos[None, :] <= highest) & (key_pos[None, :] < prompt_length...]
    add x6 -> x0, other arithmetic: 5.93 us -> none  [the longest x5 5.86 us: attend(): total = total * factor + jnp.sum(weights, axis=2)]
    dot_general x10 -> x0, matrix products: 5.45 us -> none  [the longest x5 3.75 us: attend(): jnp.einsum('shkr,skhd->shrd', weights.astype(jnp.bfloat16), value_four, p...]
    lt x6 -> x0, other arithmetic: 3.87 us -> none  [the longest x5 3.26 us: attend(): key_pos[None, :, None] < prompt_length[:, None, None]]
    another operation x6 -> x0, loops' own time: 2.56 us -> none  [the longest x1 2.24 us: shards(): lax.fori_loop(1, blocks // 2, turn, (carry, paired, paired))]
  transfers between devices with their start and end apart: 7 -> 0, of which waited for: 6 -> 0; matrix products, arithmetic and copies ran while one was open for 11% -> 0% of each run, Pallas kernels for 0% -> 0%
where the time goes in v1:
time: 25.9 us; the launch traced here: 25.7 us
  Pallas kernels  23.2 us (90%)
  local copies, waits for them, and re-layouts  1.87 us (7%)
  between operations  0.66 us (3%)
    pallas_call x1, Pallas kernels, shards(): pl.pallas_call(functools.partial(kernel, blocks, local_heads, group, span...  23.2 us
    unnamed x1, local copies, waits for them, and re-layouts  1.87 us

profile of v1, /device:TPU:0, one launch (start us, length us, event | category | flops | bytes accessed | tf_op | source)
XLA Modules:
  0.0 25.7 jit_solution(16891842642747977898)
XLA Ops:
  0.7 23.2 %shard_map.55 = bf16[1,64,4096]{2,1,0:T(8,128)(2,1)} custom-call(bf16[1,64,4096]{2,1,0:T(8,128)(2,1)} %q_hbm.1, bf16[1,64,256]{2,1,0:T(8,128)(2,1)} %k_hbm.1, bf16[1,64,256]{2,1,0:T(8,128)(2,1)} %v_hbm.1, s32[1]{0:T(128)S(6)} %copy.7.len_ref, s32[16]{0:T(128)} %order_ref.1), custom_call_target="tpu_custom_call" | custom-call | tf_op jit(solution)/shard_map/pallas_call | solution.py:164
  23.8 1.9 %copy.8 = bf16[1,64,4096]{2,1,0:T(8,128)(2,1)} copy(bf16[1,64,4096]{2,1,0:T(8,128)(2,1)} %shard_map.55) | data formatting | bytes 1048576

commit v2 on v1

--- a/solution.py
+++ b/solution.py
@@ -10,15 +10,21 @@
 
 HEAD_WIDTH = 128
 NEG_FILL = -1e30
-HEADS_PER_TILE = 4
+HEADS_PER_TILE = 2
 KEY_CHUNK = 512
 MESH = pl.DeviceIdType.MESH
 
 
+def row_length(blocks):
+    return max(d for d in range(1, math.isqrt(blocks) + 1) if blocks % d == 0)
+
+
 def kernel(
-    blocks, local_heads, group, spans, q_hbm, k_hbm, v_hbm, len_ref, order_ref, o_ref,
-    q_ref, k_ref, v_ref, bias_ref, q_sem, own_sem, send_sem, recv_sem
+    rows_z, cols_x, local_heads, group, spans, q_hbm, k_hbm, v_hbm, len_ref, order_ref, o_ref,
+    q_ref, k_ref, v_ref, bias_ref, q_sem, own_sem,
+    col_send, col_recv, row_send, row_recv
 ):
+    blocks = rows_z * cols_x
     rows = q_ref.shape[0]
     span = rows // spans
     keys = blocks * rows
@@ -31,41 +37,81 @@
     v_copy.start()
     q_copy.start()
 
-    barrier = pltpu.get_barrier_semaphore()
-    for d in range(1, blocks):
-        pl.semaphore_signal(
-            barrier, inc=1, device_id={"blk": lax.rem(me + d, blocks)}, device_id_type=MESH
-        )
-    pl.semaphore_wait(barrier, blocks - 1)
-
-    def send(ref, which, d):
+    z, x = lax.div(me, cols_x), lax.rem(me, cols_x)
+    refs = (k_ref, v_ref)
+
+    def block(row, col):
+        return pl.ds((row * cols_x + col) * rows, rows)
+
+    def wrapped(row):
+        return lax.rem(row + rows_z, rows_z)
+
+    def peer(e):
+        return z * cols_x + lax.rem(x + e, cols_x)
+
+    def copy(u, at, target, send, recv):
         return pltpu.make_async_remote_copy(
-            src_ref=ref.at[own],
-            dst_ref=ref.at[own],
-            send_sem=send_sem.at[which, d - 1],
-            recv_sem=recv_sem.at[which, d - 1],
-            device_id={"blk": lax.rem(me + d, blocks)},
+            src_ref=refs[u].at[at],
+            dst_ref=refs[u].at[at],
+            send_sem=send,
+            recv_sem=recv,
+            device_id={"blk": target},
             device_id_type=MESH,
         )
 
-    def arrival(ref, which, d):
-        source = lax.rem(me + blocks - d, blocks)
-        there = pl.ds(source * rows, rows)
-        return pltpu.make_async_remote_copy(
-            src_ref=ref.at[there],
-            dst_ref=ref.at[there],
-            send_sem=send_sem.at[which, d - 1],
-            recv_sem=recv_sem.at[which, d - 1],
-            device_id={"blk": lax.rem(me + d, blocks)},
-            device_id_type=MESH,
-        )
-
-    k_copy.wait()
-    for d in range(1, blocks):
-        send(k_ref, 0, d).start()
-    v_copy.wait()
-    for d in range(1, blocks):
-        send(v_ref, 1, d).start()
+    def to_column(row, u):
+        return copy(u, own, row * cols_x + x, col_send.at[row, u], col_recv.at[z, u])
+
+    def from_column(row, u):
+        return copy(u, block(row, x), row * cols_x + x, col_send.at[row, u], col_recv.at[row, u])
+
+    def to_row(row, e, u):
+        return copy(u, block(row, x), peer(e), row_send.at[row, e - 1, u], row_recv.at[row, e - 1, u])
+
+    def from_row(row, e, u):
+        col = lax.rem(x + cols_x - e, cols_x)
+        return copy(u, block(row, col), peer(e), row_send.at[row, e - 1, u], row_recv.at[row, e - 1, u])
+
+    def each_row(distances, visit):
+        for d in distances:
+            pl.when(z + d < rows_z)(lambda d=d: visit(z + d))
+            pl.when(z >= d)(lambda d=d: visit(z - d))
+
+    near = range(1, rows_z)
+    send_order = tuple(reversed(near))
+    barrier = pltpu.get_barrier_semaphore()
+
+    def greet(target):
+        pl.semaphore_signal(barrier, inc=1, device_id={"blk": target}, device_id_type=MESH)
+
+    for d in near:
+        greet(lax.rem(me + d * cols_x, blocks))
+    for e in range(1, cols_x):
+        greet(peer(e))
+    pl.semaphore_wait(barrier, rows_z + cols_x - 2)
+
+    for u, own_copy in enumerate((k_copy, v_copy)):
+        own_copy.wait()
+        each_row(send_order, lambda row, u=u: to_column(row, u).start())
+        for e in range(1, cols_x):
+            to_row(z, e, u).start()
+
+    def relay(row, u):
+        from_column(row, u).wait_recv()
+        for e in range(1, cols_x):
+            to_row(row, e, u).start()
+
+    def gather_row(row, u):
+        for e in range(1, cols_x):
+            from_row(row, e, u).wait_recv()
+
+    def drain():
+        for u in range(2):
+            for d in near:
+                to_column(lax.rem(z + d, rows_z), u).wait_send()
+            for row in range(rows_z):
+                for e in range(1, cols_x):
+                    to_row(row, e, u).wait_send()
 
     limit = len_ref[0]
     row = lax.broadcasted_iota(jnp.int32, (rows, 1), 0)
@@ -89,9 +135,11 @@
     live = row_pos < limit
     q_copy.wait()
 
-    for which, ref in ((0, k_ref), (1, v_ref)):
-        for d in range(1, blocks):
-            arrival(ref, which, d).wait_recv()
+    for u in range(2):
+        each_row(tuple(reversed(near)), lambda row, u=u: relay(row, u))
+    for u in range(2):
+        for row in range(rows_z):
+            gather_row(row, u)
 
     scale = HEAD_WIDTH ** (-0.5) * math.log2(math.e)
     tile = HEADS_PER_TILE if group % HEADS_PER_TILE == 0 else 1
@@ -142,15 +190,15 @@
                 piece = jnp.where(live, out[t * rows : (t + 1) * rows], 0.0)
                 o_ref[0, :, q_cols(t)] = piece.astype(o_ref.dtype)
 
-        pl.loop(0, group // tile)(run_tile)
-
-    for which, ref in ((0, k_ref), (1, v_ref)):
-        for d in range(1, blocks):
-            send(ref, which, d).wait_send()
+        pl.loop(0, group // tile, unroll=True)(run_tile)
+
+    drain()
 
 
 def solution(mesh):
     blocks = mesh.shape["blk"]
+    cols_x = row_length(blocks)
+    rows_z = blocks // cols_x
 
     def shards(queries, keys, values, prompt_length, span_order):
         _, rows, width = queries.shape
@@ -159,10 +207,11 @@
         group = width // kv_width
         total = blocks * rows
         chunk = min(total, KEY_CHUNK)
+        held = rows * width * 2 + total * kv_width * 4 + total * rows * 4
         anywhere = pl.BlockSpec(memory_space=pl.ANY)
         scalars = pl.BlockSpec(memory_space=pltpu.SMEM)
         return pl.pallas_call(
-            functools.partial(kernel, blocks, local_heads, group, span_order.shape[0] // blocks),
+            functools.partial(kernel, rows_z, cols_x, local_heads, group, span_order.shape[0] // blocks),
             out_shape=jax.ShapeDtypeStruct(queries.shape, queries.dtype),
             in_specs=[anywhere, anywhere, anywhere, scalars, scalars],
             out_specs=pl.BlockSpec(memory_space=pltpu.VMEM),
@@ -173,11 +222,11 @@
                 pltpu.VMEM((total // chunk, rows, chunk), jnp.float32),
                 pltpu.SemaphoreType.DMA,
                 pltpu.SemaphoreType.DMA((2,)),
-                pltpu.SemaphoreType.DMA((2, blocks - 1)),
-                pltpu.SemaphoreType.DMA((2, blocks - 1)),
+                *[pltpu.SemaphoreType.DMA((rows_z, 2))] * 2,
+                *[pltpu.SemaphoreType.DMA((rows_z, cols_x, 2))] * 2,
             ],
             compiler_params=pltpu.CompilerParams(
-                collective_id=0, has_side_effects=True, vmem_limit_bytes=56 * 1024 * 1024
+                collective_id=0, has_side_effects=True, vmem_limit_bytes=held + 6 * 1024 * 1024
             ),
         )(queries, keys, values, prompt_length, span_order)
 

time: 25.9 us -> 22.1 us (0.85)
  Pallas kernels: 23.2 us -> 17.7 us
  local copies, waits for them, and re-layouts: 1.87 us -> 3.35 us
    pallas_call x1, Pallas kernels: 23.2 us -> 17.7 us  [shards(): pl.pallas_call(functools.partial(kernel, rows_z, cols_x, local_heads, gro...]
    unnamed x1 -> x9, local copies, waits for them, and re-layouts: 1.87 us -> 3.35 us
where the time goes in v2:
time: 22.1 us; the launch traced here: 21.8 us
  Pallas kernels  17.7 us (80%)
  local copies, waits for them, and re-layouts  3.35 us (15%)
  between operations  0.69 us (3%)
    pallas_call x1, Pallas kernels, shards(): pl.pallas_call(functools.partial(kernel, rows_z, cols_x, local_heads, gro...  17.7 us
    unnamed x9, local copies, waits for them, and re-layouts  3.35 us

profile of v2, /device:TPU:0, one launch (start us, length us, event | category | flops | bytes accessed | tf_op | source)
XLA Modules:
  0.0 21.8 jit_solution(15923988201915386749)
XLA Ops:
  0.0 0.0 copy-start.3
  0.7 0.0 copy-done.3
  0.7 0.0 copy-start
  0.7 1.0 %copy-done = bf16[1,64,4096]{2,1,0:T(8,128)(2,1)S(1)} copy-done((bf16[1,64,4096]{2,1,0:T(8,128)(2,1)S(1)}, bf16[1,64,4096]{2,1,0:T(8,128)(2,1)}, u32[]{:S(2)}) %copy-start) | copy-done | bytes 524312
  1.7 0.0 copy-start.1
  1.7 0.8 %copy-done.1 = bf16[1,64,256]{2,1,0:T(8,128)(2,1)S(1)} copy-done((bf16[1,64,256]{2,1,0:T(8,128)(2,1)S(1)}, bf16[1,64,256]{2,1,0:T(8,128)(2,1)}, u32[]{:S(2)}) %copy-start.1) | copy-done | bytes 32792
  2.5 0.0 copy-start.2
  2.5 0.8 %copy-done.2 = bf16[1,64,256]{2,1,0:T(8,128)(2,1)S(1)} copy-done((bf16[1,64,256]{2,1,0:T(8,128)(2,1)S(1)}, bf16[1,64,256]{2,1,0:T(8,128)(2,1)}, u32[]{:S(2)}) %copy-start.2) | copy-done | bytes 32792
  3.2 17.7 %shard_map.55 = bf16[1,64,4096]{2,1,0:T(8,128)(2,1)S(1)} custom-call(bf16[1,64,4096]{2,1,0:T(8,128)(2,1)S(1)} %copy-done, bf16[1,64,256]{2,1,0:T(8,128)(2,1)S(1)} %copy-done.1, bf16[1,64,256]{2,1,0:T(8,128)(2,1)S(1)} %copy-done.2, s32[1]{0:T(128)S(6)} %copy.7.len_ref, s32[16]{0:T(128)S(1)} %copy-done.3), custom_call_target="tpu_custom_call" | custom-call | tf_op jit(solution)/shard_map/pallas_call | solution.py:213
  21.0 0.8 %copy.8 = bf16[1,64,4096]{2,1,0:T(8,128)(2,1)} copy(bf16[1,64,4096]{2,1,0:T(8,128)(2,1)S(1)} %shard_map.55) | data formatting | bytes 1048576
Async XLA Ops:
  0.0 0.7 %copy-start.3 = (s32[16]{0:T(128)S(1)}, s32[16]{0:T(128)}, u32[]{:S(2)}) copy-start(s32[16]{0:T(128)} %order_ref.1) | copy-start | bytes 196
  0.7 1.0 %copy-start = (bf16[1,64,4096]{2,1,0:T(8,128)(2,1)S(1)}, bf16[1,64,4096]{2,1,0:T(8,128)(2,1)}, u32[]{:S(2)}) copy-start(bf16[1,64,4096]{2,1,0:T(8,128)(2,1)} %q_hbm.1) | copy-start | bytes 1572868
  1.7 0.8 %copy-start.1 = (bf16[1,64,256]{2,1,0:T(8,128)(2,1)S(1)}, bf16[1,64,256]{2,1,0:T(8,128)(2,1)}, u32[]{:S(2)}) copy-start(bf16[1,64,256]{2,1,0:T(8,128)(2,1)} %k_hbm.1) | copy-start | bytes 98308
  2.5 0.8 %copy-start.2 = (bf16[1,64,256]{2,1,0:T(8,128)(2,1)S(1)}, bf16[1,64,256]{2,1,0:T(8,128)(2,1)}, u32[]{:S(2)}) copy-start(bf16[1,64,256]{2,1,0:T(8,128)(2,1)} %v_hbm.1) | copy-start | bytes 98308

commit v3 on v2

--- a/solution.py
+++ b/solution.py
@@ -12,6 +12,8 @@
 NEG_FILL = -1e30
 HEADS_PER_TILE = 2
 KEY_CHUNK = 512
+OUT_PARTS = 2
+VMEM_LIMIT = 56 * 1024 * 1024
 MESH = pl.DeviceIdType.MESH
 
 
@@ -20,8 +22,8 @@
 
 
 def kernel(
-    rows_z, cols_x, local_heads, group, spans, q_hbm, k_hbm, v_hbm, len_ref, order_ref, o_ref,
-    q_ref, k_ref, v_ref, bias_ref, q_sem, own_sem,
+    rows_z, cols_x, local_heads, group, spans, q_hbm, k_hbm, v_hbm, len_hbm, order_hbm, o_hbm,
+    q_ref, o_ref, k_ref, v_ref, bias_ref, len_ref, order_ref, q_sem, own_sem, small_sem, out_sem,
     col_send, col_recv, row_send, row_recv
 ):
     blocks = rows_z * cols_x
@@ -36,6 +38,10 @@
     k_copy.start()
     v_copy.start()
     q_copy.start()
+    len_copy = pltpu.make_async_copy(len_hbm, len_ref, small_sem.at[0])
+    order_copy = pltpu.make_async_copy(order_hbm, order_ref, small_sem.at[1])
+    len_copy.start()
+    order_copy.start()
 
     z, x = lax.div(me, cols_x), lax.rem(me, cols_x)
     refs = (k_ref, v_ref)
@@ -113,6 +119,8 @@
                 for e in range(1, cols_x):
                     to_row(row, e, u).wait_send()
 
+    len_copy.wait()
+    order_copy.wait()
     limit = len_ref[0]
     row = lax.broadcasted_iota(jnp.int32, (rows, 1), 0)
     row_pos = jnp.zeros((rows, 1), jnp.int32)
@@ -146,6 +154,11 @@
     height = tile * rows
     ones = jnp.ones((chunk, HEAD_WIDTH), jnp.bfloat16)
 
+    def out_copy(h, p):
+        wide = group * HEAD_WIDTH // OUT_PARTS
+        at = pl.ds((h * OUT_PARTS + p) * wide, wide)
+        return pltpu.make_async_copy(o_ref.at[:, at], o_hbm.at[0, :, at], out_sem.at[h, p])
+
     for h in range(local_heads):
         cols = slice(h * HEAD_WIDTH, (h + 1) * HEAD_WIDTH)
 
@@ -188,11 +201,18 @@
             out = mixed[:, :HEAD_WIDTH] / mixed[:, HEAD_WIDTH:]
             for t in range(tile):
                 piece = jnp.where(live, out[t * rows : (t + 1) * rows], 0.0)
-                o_ref[0, :, q_cols(t)] = piece.astype(o_ref.dtype)
-
-        pl.loop(0, group // tile, unroll=True)(run_tile)
+                o_ref[:, q_cols(t)] = piece.astype(o_ref.dtype)
+
+        tiles = group // tile
+        per_part = tiles // OUT_PARTS
+        for p in range(OUT_PARTS):
+            pl.loop(p * per_part, (p + 1) * per_part, unroll=True)(run_tile)
+            out_copy(h, p).start()
 
     drain()
+    for h in range(local_heads):
+        for p in range(OUT_PARTS):
+            out_copy(h, p).wait()
 
 
 def solution(mesh):
@@ -207,26 +227,28 @@
         group = width // kv_width
         total = blocks * rows
         chunk = min(total, KEY_CHUNK)
-        held = rows * width * 2 + total * kv_width * 4 + total * rows * 4
-        anywhere = pl.BlockSpec(memory_space=pl.ANY)
-        scalars = pl.BlockSpec(memory_space=pltpu.SMEM)
+        anywhere = pl.BlockSpec(memory_space=pltpu.HBM)
         return pl.pallas_call(
             functools.partial(kernel, rows_z, cols_x, local_heads, group, span_order.shape[0] // blocks),
             out_shape=jax.ShapeDtypeStruct(queries.shape, queries.dtype),
-            in_specs=[anywhere, anywhere, anywhere, scalars, scalars],
-            out_specs=pl.BlockSpec(memory_space=pltpu.VMEM),
+            in_specs=[anywhere] * 5,
+            out_specs=anywhere,
             scratch_shapes=[
-                pltpu.VMEM((rows, width), queries.dtype),
+                *[pltpu.VMEM((rows, width), queries.dtype)] * 2,
                 pltpu.VMEM((total, kv_width), keys.dtype),
                 pltpu.VMEM((total, kv_width), values.dtype),
                 pltpu.VMEM((total // chunk, rows, chunk), jnp.float32),
+                pltpu.SMEM(prompt_length.shape, jnp.int32),
+                pltpu.SMEM(span_order.shape, jnp.int32),
                 pltpu.SemaphoreType.DMA,
                 pltpu.SemaphoreType.DMA((2,)),
+                pltpu.SemaphoreType.DMA((2,)),
+                pltpu.SemaphoreType.DMA((local_heads, OUT_PARTS)),
                 *[pltpu.SemaphoreType.DMA((rows_z, 2))] * 2,
                 *[pltpu.SemaphoreType.DMA((rows_z, cols_x, 2))] * 2,
             ],
             compiler_params=pltpu.CompilerParams(
-                collective_id=0, has_side_effects=True, vmem_limit_bytes=held + 6 * 1024 * 1024
+                collective_id=0, has_side_effects=True, vmem_limit_bytes=VMEM_LIMIT
             ),
         )(queries, keys, values, prompt_length, span_order)
 

time: 22.1 us -> 20.5 us (0.928)
  local copies, waits for them, and re-layouts: 3.35 us -> 1.87 us
    unnamed x9 -> x1, local copies, waits for them, and re-layouts: 3.35 us -> 1.87 us
where the time goes in v3:
time: 20.5 us; the launch traced here: 20.3 us
  Pallas kernels  17.8 us (87%)
  local copies, waits for them, and re-layouts  1.87 us (9%)
  between operations  0.66 us (3%)
    pallas_call x1, Pallas kernels, shards(): pl.pallas_call(functools.partial(kernel, rows_z, cols_x, local_heads, gro...  17.8 us
    unnamed x1, local copies, waits for them, and re-layouts  1.87 us

profile of v3, /device:TPU:0, one launch (start us, length us, event | category | flops | bytes accessed | tf_op | source)
XLA Modules:
  0.0 20.3 jit_solution(13447107286298161482)
XLA Ops:
  0.7 17.8 %shard_map.55 = bf16[1,64,4096]{2,1,0:T(8,128)(2,1)} custom-call(bf16[1,64,4096]{2,1,0:T(8,128)(2,1)} %q_hbm.1, bf16[1,64,256]{2,1,0:T(8,128)(2,1)} %k_hbm.1, bf16[1,64,256]{2,1,0:T(8,128)(2,1)} %v_hbm.1, s32[1]{0:T(128)S(6)} %copy.7.len_hbm, s32[16]{0:T(128)} %order_hbm.1), custom_call_target="tpu_custom_call" | custom-call | tf_op jit(solution)/shard_map/pallas_call | solution.py:231
  18.5 1.9 %copy.8 = bf16[1,64,4096]{2,1,0:T(8,128)(2,1)} copy(bf16[1,64,4096]{2,1,0:T(8,128)(2,1)} %shard_map.55) | data formatting | bytes 1048576

commit v4 on v3

--- a/solution.py
+++ b/solution.py
@@ -23,7 +23,7 @@
 
 def kernel(
     rows_z, cols_x, local_heads, group, spans, q_hbm, k_hbm, v_hbm, len_hbm, order_hbm, o_hbm,
-    q_ref, o_ref, k_ref, v_ref, bias_ref, len_ref, order_ref, q_sem, own_sem, small_sem, out_sem,
+    q_ref, o_ref, k_ref, v_ref, bias_ref, w_ref, len_ref, order_ref, q_sem, own_sem, small_sem, out_sem,
     col_send, col_recv, row_send, row_recv
 ):
     blocks = rows_z * cols_x
@@ -145,9 +145,12 @@
 
     for u in range(2):
         each_row(tuple(reversed(near)), lambda row, u=u: relay(row, u))
-    for u in range(2):
+    for row in range(rows_z):
+        gather_row(row, 0)
+
+    def gather_values():
         for row in range(rows_z):
-            gather_row(row, u)
+            gather_row(row, 1)
 
     scale = HEAD_WIDTH ** (-0.5) * math.log2(math.e)
     tile = HEADS_PER_TILE if group % HEADS_PER_TILE == 0 else 1
@@ -159,35 +162,47 @@
         at = pl.ds((h * OUT_PARTS + p) * wide, wide)
         return pltpu.make_async_copy(o_ref.at[:, at], o_hbm.at[0, :, at], out_sem.at[h, p])
 
-    for h in range(local_heads):
+    if chunks > 1:
+        gather_values()
+
+    for phase, h in [(p, h) for p in range(2 if chunks == 1 else 1) for h in range(local_heads)]:
+        if phase == 1 and h == 0:
+            gather_values()
         cols = slice(h * HEAD_WIDTH, (h + 1) * HEAD_WIDTH)
 
-        def run_tile(i, h=h, cols=cols):
+        def run_tile(i, h=h, cols=cols, phase=phase):
             first = h * group * HEAD_WIDTH + i * (tile * HEAD_WIDTH)
 
             def q_cols(t):
                 return pl.ds(pl.multiple_of(first + t * HEAD_WIDTH, HEAD_WIDTH), HEAD_WIDTH)
 
+            kept = pl.ds(pl.multiple_of((h * (group // tile) + i) * height, height), height)
             q = jnp.concatenate([q_ref[:, q_cols(t)] for t in range(tile)], axis=0)
 
-            def part(c):
+            def score_of(c):
                 at = pl.ds(pl.multiple_of(c * chunk, chunk), chunk)
                 score = lax.dot_general(
                     q, k_ref[at, cols], (((1,), (1,)), ((), ())), preferred_element_type=jnp.float32
                 )
                 score = (score * scale).reshape(tile, rows, chunk) + bias_ref[c][None]
-                return score.reshape(height, chunk), jnp.concatenate([v_ref[at, cols], ones], axis=1)
-
+                return score.reshape(height, chunk)
+
+            def value_of(c):
+                at = pl.ds(pl.multiple_of(c * chunk, chunk), chunk)
+                return jnp.concatenate([v_ref[at, cols], ones], axis=1)
+
+            if chunks == 1 and phase == 0:
+                score = score_of(0)
+                top = jnp.max(score, axis=1, keepdims=True)
+                w_ref[kept] = jnp.exp2(score - top).astype(jnp.bfloat16)
+                return
             if chunks == 1:
-                score, value = part(0)
-                top = jnp.max(score, axis=1, keepdims=True)
-                weight = jnp.exp2(score - top).astype(jnp.bfloat16)
-                mixed = jnp.dot(weight, value, preferred_element_type=jnp.float32)
+                mixed = jnp.dot(w_ref[kept], value_of(0), preferred_element_type=jnp.float32)
             else:
 
                 def step(c, state):
                     best, mixed = state
-                    score, value = part(c)
+                    score, value = score_of(c), value_of(c)
                     top = jnp.maximum(best, jnp.max(score, axis=1, keepdims=True))
                     weight = jnp.exp2(score - top).astype(jnp.bfloat16)
                     fresh = jnp.dot(weight, value, preferred_element_type=jnp.float32)
@@ -207,7 +222,8 @@
         per_part = tiles // OUT_PARTS
         for p in range(OUT_PARTS):
             pl.loop(p * per_part, (p + 1) * per_part, unroll=True)(run_tile)
-            out_copy(h, p).start()
+            if phase == 1 or chunks > 1:
+                out_copy(h, p).start()
 
     drain()
     for h in range(local_heads):
@@ -238,6 +254,7 @@
                 pltpu.VMEM((total, kv_width), keys.dtype),
                 pltpu.VMEM((total, kv_width), values.dtype),
                 pltpu.VMEM((total // chunk, rows, chunk), jnp.float32),
+                pltpu.VMEM((local_heads * group * rows if chunk == total else rows, chunk), jnp.bfloat16),
                 pltpu.SMEM(prompt_length.shape, jnp.int32),
                 pltpu.SMEM(span_order.shape, jnp.int32),
                 pltpu.SemaphoreType.DMA,

time: 20.5 us -> 19.7 us (0.961)
  Pallas kernels: 17.8 us -> 17 us
    pallas_call x1, Pallas kernels: 17.8 us -> 17 us  [shards(): pl.pallas_call(functools.partial(kernel, rows_z, cols_x, local_heads, gro...]
where the time goes in v4:
time: 19.7 us; the launch traced here: 19.5 us
  Pallas kernels  17 us (86%)
  local copies, waits for them, and re-layouts  1.87 us (9%)
  between operations  0.66 us (3%)
    pallas_call x1, Pallas kernels, shards(): pl.pallas_call(functools.partial(kernel, rows_z, cols_x, local_heads, gro...  17 us
    unnamed x1, local copies, waits for them, and re-layouts  1.87 us

profile of v4, /device:TPU:0, one launch (start us, length us, event | category | flops | bytes accessed | tf_op | source)
XLA Modules:
  0.0 19.5 jit_solution(4242067515717406178)
XLA Ops:
  0.7 17.0 %shard_map.55 = bf16[1,64,4096]{2,1,0:T(8,128)(2,1)} custom-call(bf16[1,64,4096]{2,1,0:T(8,128)(2,1)} %q_hbm.1, bf16[1,64,256]{2,1,0:T(8,128)(2,1)} %k_hbm.1, bf16[1,64,256]{2,1,0:T(8,128)(2,1)} %v_hbm.1, s32[1]{0:T(128)S(6)} %copy.7.len_hbm, s32[16]{0:T(128)} %order_hbm.1), custom_call_target="tpu_custom_call" | custom-call | tf_op jit(solution)/shard_map/pallas_call | solution.py:247
  17.7 1.9 %copy.8 = bf16[1,64,4096]{2,1,0:T(8,128)(2,1)} copy(bf16[1,64,4096]{2,1,0:T(8,128)(2,1)} %shard_map.55) | data formatting | bytes 1048576
